TPU v7x, 32 devices: a whole 2x2x4 slice. The times are simulated.
32 devices in a mesh: blk: 16 (over z, x, core), rep: 2 (over y).
Axes of the slice: x: 2, y: 2, z: 4, core: 2. Of those that a mesh axis runs over, the one named last changes fastest.
Arguments:
- captions: bfloat16 [6144, 768], P(('blk', 'rep')), may hold values from -512 to 512
- images: bfloat16 [6144, 768], P(('blk', 'rep')), may hold values from -512 to 512
- positives: int32 [6144], P(('blk', 'rep')), may hold values from 0 to 6143, each once
- valid: int32 [6144], P(('blk', 'rep')), may hold values from 0 to 1, as said below
Outputs:
- caption_loss: float32 [6144], P(('blk', 'rep'))
- image_loss: float32 [6144], P(('blk', 'rep'))
- loss: float32 [], replicated
Inputs may be any that keep to these rules, and one draw needn't show every extreme that they name: `positives`: each image row is the positive of exactly one caption; a program may pack several of these indices into one sent element. `valid`: the last image row is always real; a program may pack several of these flags into one sent element.
All inputs are finite; a program needn't handle non-finite values.
Results may differ from a plain program's by a relative error of at most 0.0003.
Values may be sent and summed in bfloat16 or wider, within the bound.
A program may use at most 128 MiB of HBM per device.

v0:
```python
import jax
import jax.numpy as jnp
from jax import lax
from jax.sharding import PartitionSpec as P

very_low = -1e30


def merged(part, axis, combine):
    gathered = jax.tree.map(lambda a: lax.all_gather(a, axis), part)

    def take(source):
        return jax.tree.map(lambda a: lax.dynamic_index_in_dim(a, source, 0, False), gathered)

    return lax.fori_loop(
        1, lax.axis_size(axis), lambda source, state: combine(state, take(source)), take(0)
    )


def fold_rows(running, scores, image_ok, is_positive):
    row_peak, row_total, row_match = running
    usable = image_ok[None, :] > 0
    highest = jnp.max(jnp.where(usable, scores, very_low), axis=1)
    renewed = jnp.maximum(row_peak, highest)
    powers = jnp.where(usable, jnp.exp(scores - renewed[:, None]), 0.0)
    row_total = jnp.sum(powers, axis=1)
    row_match = jnp.sum(jnp.where(is_positive, scores, 0.0), axis=1)
    return (renewed, row_total, row_match)


def fold_columns(running, scores, caption_live, is_positive):
    column_peak, column_total, column_match = running
    highest = jnp.max(jnp.where(caption_live, scores, very_low), axis=0)
    renewed = jnp.maximum(column_peak, highest)
    powers = jnp.where(caption_live, jnp.exp(scores - renewed[None, :]), 0.0)
    column_total = jnp.sum(powers, axis=0)
    column_match = jnp.sum(jnp.where(is_positive, scores, 0.0), axis=0)
    return (renewed, column_total, column_match)


def join_parts(first, second):
    peak_first, total_first, match_first = first
    peak_second, total_second, match_second = second
    highest = jnp.maximum(peak_first, peak_second)
    merged_total = total_first * jnp.exp(peak_first - highest) + total_second * jnp.exp(
        peak_second - highest
    )
    return (highest, merged_total, match_first + match_second)


def empty_columns(length):
    return (
        jnp.full((length,), very_low, jnp.float32),
        jnp.zeros((length,), jnp.float32),
        jnp.zeros((length,), jnp.float32),
    )


def local(captions, images, positives, valid):
    row_count = captions.shape[0]
    cycle_index = lax.axis_index("blk")
    pair_index = lax.axis_index("rep")
    image_flags = lax.all_gather(valid, ("blk", "rep"), axis=0, tiled=True).astype(jnp.float32)
    caption_ok = jnp.take(image_flags, positives, axis=0)
    image_block = lax.all_gather(images, "rep", axis=0, tiled=True)
    block_rows = image_block.shape[0]
    own_ok = lax.dynamic_slice_in_dim(
        image_flags, cycle_index * block_rows + pair_index * row_count, row_count
    )
    all_targets = lax.all_gather(positives, "blk", axis=0, tiled=True)
    image_start = cycle_index * block_rows
    block_ok = lax.dynamic_slice_in_dim(image_flags, image_start, block_rows)
    image_ids = image_start + lax.iota(jnp.int32, block_rows)
    piece = lax.all_gather(captions, "blk", axis=0, tiled=True)
    column_parts = empty_columns(block_rows)
    piece_count = piece.shape[0]
    piece_ok = jnp.take(image_flags, all_targets, axis=0)
    scores = lax.dot_general(
        piece, image_block, (((1,), (1,)), ((), ())), preferred_element_type=jnp.float32
    )
    is_positive = all_targets[:, None] == image_ids[None, :]
    fresh = fold_rows(empty_columns(piece_count), scores, block_ok, is_positive)
    row_parts = tuple((part for part in fresh))
    column_parts = fold_columns(column_parts, scores, piece_ok[:, None] > 0, is_positive)
    row_parts, column_parts = (row_parts, tuple(column_parts))
    row_joined = merged((row_parts[0], row_parts[1], row_parts[2]), "blk", join_parts)
    row_state = tuple(
        (
            lax.dynamic_slice_in_dim(column, cycle_index * row_count, row_count)
            for column in row_joined
        )
    )
    column_joined = merged((column_parts[0], column_parts[1], column_parts[2]), "rep", join_parts)
    own_columns = tuple(
        (
            lax.dynamic_slice_in_dim(column, pair_index * row_count, row_count)
            for column in column_joined
        )
    )
    caption_loss = caption_ok * (row_state[0] + jnp.log(row_state[1]) - row_state[2])
    image_loss = own_ok * (own_columns[0] + jnp.log(own_columns[1]) - own_columns[2])
    totals = lax.psum((jnp.sum(caption_loss), jnp.sum(image_loss)), ("blk", "rep"))
    loss = (totals[0] + totals[1]) / (2.0 * jnp.sum(image_flags))
    return (caption_loss, image_loss, loss)


def solution(mesh):
    placed = (
        P(("blk", "rep"), None),
        P(("blk", "rep"), None),
        P(("blk", "rep")),
        P(("blk", "rep")),
    )
    return jax.shard_map(
        local,
        mesh=mesh,
        in_specs=placed,
        out_specs=(P(("blk", "rep")), P(("blk", "rep")), P()),
        check_vma=False,
    )
```

profile of v0, /device:TPU:0, one launch (start us, length us, event | category | flops | bytes accessed | tf_op | source)
XLA Modules:
  0.0 277.1 jit_solution(10429886929152624074)
XLA Ops:
  7.2 0.7 all-gather.11.cloned.1.call-update
  7.9 1.2 dynamic-slice.2
  9.2 0.9 dynamic-update-slice
  10.0 44.2 %all-reduce = s32[6144]{0:T(1024)S(1)} all-reduce(s32[6144]{0:T(1024)S(1)} %dynamic-update-slice), channel_id=1, replica_groups=mesh['blk'=16,'rep'=2] {'blk','rep'}, use_global_device_ids=true, to_apply=%add | all-reduce | flops 6144 | bytes 49152
  54.9 0.9 dynamic-update-slice.1
  55.8 0.7 compare_select_fusion.2
  56.4 1.4 gather_fusion
  57.9 58.6 %all-reduce.1 = s32[3072]{0:T(1024)S(1)} all-reduce(s32[3072]{0:T(1024)S(1)} %dynamic-update-slice.1), channel_id=1, replica_groups=mesh['blk'=16,'rep'=2] {'blk'}, use_global_device_ids=true, to_apply=%add.1 | all-reduce | flops 3072 | bytes 24576
  116.5 17.4 %gather_fusion.1 = f32[3072]{0:T(1024)S(1)} fusion(f32[6144]{0:T(1024)S(1)} %convert_element_type.3, s32[3072]{0:T(1024)S(1)} %fusion.2), kind=kCustom, calls=%fused_computation.1 | custom fusion | bytes 36864 | tf_op jit(solution)/shard_map/jit(_take)/gather | solution.py:77
  133.9 0.1 dynamic-slice_compare_fusion
  134.0 0.7 convert_reduce_fusion
  134.7 7.4 %all_gather.46 = bf16[384,768]{1,0:T(8,128)(2,1)S(1)} all-gather(bf16[192,768]{1,0:T(8,128)(2,1)S(1)} %copy-done.1), channel_id=1, replica_groups=mesh['blk'=16,'rep'=2] {'rep'}, dimensions={0}, use_global_device_ids=true | all-gather | bytes 884736 | tf_op jit(solution)/shard_map/all_gather | solution.py:65
  142.1 7.2 %select_reduce_fusion.3 = (f32[3072]{0:T(1024)S(1)}, f32[3072,384]{1,0:T(8,128)}) fusion(pred[384]{0:T(512)(128)(4,1)S(1)} %dynamic-slice_compare_fusion, bf16[3072,768]{1,0:T(8,128)(2,1)} %all-gather.11.cloned.1.call-done, bf16[384,768]{1,0:T(8,128)(2,1)S(1)} %all_gather.46), kind=kOutput, calls=%fused_computation.9 | convolution fusion | flops 1814295552 | bytes 10039680 | tf_op jit(solution)/shard_map/dot_general | solution.py:78
  149.2 17.6 %all-gather = f32[49152]{0:T(1024)S(1)} all-gather(f32[3072]{0:T(1024)S(1)} %broadcast_maximum_fusion), channel_id=2, replica_groups=mesh['blk'=16,'rep'=2] {'blk'}, dimensions={0}, use_global_device_ids=true | all-gather | bytes 208896 | tf_op jit(solution)/shard_map/all_gather | solution.py:10
  166.9 4.3 %select_reduce_fusion.1 = (f32[384]{0:T(512)S(1)}, f32[3072]{0:T(1024)S(1)}) fusion(f32[3072,384]{1,0:T(8,128)} %get-tuple-element.244, pred[3072]{0:T(1024)(128)(4,1)S(1)} %select_compare_fusion, f32[3072]{0:T(1024)S(1)} %broadcast_maximum_fusion, pred[384]{0:T(512)(128)(4,1)S(1)} %dynamic-slice_compare_fusion), kind=kLoop, calls=%fused_computation.7 | loop fusion | flops 5894784 | bytes 4748160 | tf_op jit(solution)/shard_map/reduce_max | solution.py:33
  171.3 2.7 fusion
  174.0 19.7 %all-gather.2 = f32[49152]{0:T(1024)S(1)} all-gather(f32[3072]{0:T(1024)S(1)} %get-tuple-element.209), channel_id=4, replica_groups=mesh['blk'=16,'rep'=2] {'blk'}, dimensions={0}, use_global_device_ids=true | all-gather | bytes 208896 | tf_op jit(solution)/shard_map/all_gather | solution.py:10
  193.7 18.0 %all-gather.1 = f32[49152]{0:T(1024)S(1)} all-gather(f32[3072]{0:T(1024)S(1)} %get-tuple-element.212), channel_id=3, replica_groups=mesh['blk'=16,'rep'=2] {'blk'}, dimensions={0}, use_global_device_ids=true | all-gather | bytes 208896 | tf_op jit(solution)/shard_map/all_gather | solution.py:10
  211.7 4.4 %all-gather.8 = f32[2,1,384]{2,1,0:T(1,128)S(1)} all-gather(f32[1,1,384]{2,1,0:T(1,128)S(1)} %reshape.102), channel_id=7, replica_groups=mesh['blk'=16,'rep'=2] {'rep'}, dimensions={0}, use_global_device_ids=true | all-gather | bytes 4608 | tf_op jit(solution)/shard_map/all_gather | solution.py:10
  216.1 4.4 %all-gather.7 = f32[2,1,384]{2,1,0:T(1,128)S(1)} all-gather(f32[1,1,384]{2,1,0:T(1,128)S(1)} %reshape.100), channel_id=6, replica_groups=mesh['blk'=16,'rep'=2] {'rep'}, dimensions={0}, use_global_device_ids=true | all-gather | bytes 4608 | tf_op jit(solution)/shard_map/all_gather | solution.py:10
  220.5 4.4 %all-gather.6 = f32[2,1,384]{2,1,0:T(1,128)S(1)} all-gather(f32[1,1,384]{2,1,0:T(1,128)S(1)} %reshape.98), channel_id=5, replica_groups=mesh['blk'=16,'rep'=2] {'rep'}, dimensions={0}, use_global_device_ids=true | all-gather | bytes 4608 | tf_op jit(solution)/shard_map/all_gather | solution.py:10
  224.8 1.7 while.12
  226.7 1.3 fusion.4
  230.0 38.5 %psum.16 = f32[]{:T(128)} all-reduce(f32[]{:T(128)S(6)} %add.153), channel_id=1, replica_groups=mesh['blk'=16,'rep'=2] {'blk','rep'}, use_global_device_ids=true, to_apply=%region_9.10 | all-reduce | flops 1 | bytes 8 | tf_op jit(solution)/shard_map/psum | solution.py:102
  (91 shorter events, 1.4 us)
Async XLA Ops:
  7.2 134.9 %all-gather.11.cloned.1.call-start = ((), (), s32[]{:S(2)}) async-start(), calls=%async_computation | async-start | bytes 5013504 | tf_op jit(solution)/shard_map/all_gather | solution.py:74
  116.5 18.2 %copy-start.1 = (bf16[192,768]{1,0:T(8,128)(2,1)S(1)}, bf16[192,768]{1,0:T(8,128)(2,1)}, u32[]{:S(2)}) copy-start(bf16[192,768]{1,0:T(8,128)(2,1)} %param.7) | copy-start | bytes 884740
  166.9 4.4 %copy-start = (f32[3072,384]{1,0:T(8,128)S(1)}, f32[3072,384]{1,0:T(8,128)}, u32[]{:S(2)}) copy-start(f32[3072,384]{1,0:T(8,128)} %get-tuple-element.244) | copy-start | bytes 14155780
  171.3 55.4 %copy-start.2 = (s32[192]{0:T(256)S(1)}, s32[192]{0:T(256)}, u32[]{:S(2)}) copy-start(s32[192]{0:T(256)} %param.8) | copy-start | bytes 2308
Sparse Core Ops, SparseCore 0:
  10.3 56.5 all-gather.10
where the time goes:
time: 279 us; the launch traced here: 277 us
  blocking collectives  217 us (78%)
  local copies, waits for them, and re-layouts  22.7 us (8%)
  between operations  18.6 us (7%)
  other arithmetic  10.2 us (4%)
  matrix products  7.15 us (3%)
    unnamed x2, blocking collectives  103 us
    all_gather x6, blocking collectives, merged(): gathered = jax.tree.map(lambda a: lax.all_gather(a, axis), part)  68.3 us
    psum x1, blocking collectives, local(): lax.psum((jnp.sum(caption_loss), jnp.sum(image_loss)), ('blk', 'rep'))  38.5 us
    gather x1, local copies, waits for them, and re-layouts, local(): piece_ok = jnp.take(image_flags, all_targets, axis=0)  17.4 us
    all_gather x1, blocking collectives, local(): image_block = lax.all_gather(images, 'rep', axis=0, tiled=True)  7.38 us
    dot_general x1, matrix products, local(): lax.dot_general(piece, image_block, (((1,), (1,)), ((), ())), preferred_e...  7.15 us
  transfers between devices with their start and end apart: 1, of which 0 were waited for; matrix products, arithmetic and copies ran while one was open for 8% of the time, Pallas kernels for 0%

commit v1 on v0

v1 whole, which is shorter than its diff:
```python
import functools

import jax
import jax.numpy as jnp
from jax import lax
from jax.experimental import pallas as pl
from jax.experimental.pallas import tpu as pltpu
from jax.sharding import PartitionSpec as P

very_low = -1e30
floor = -1e29
PIECES = 2


def grid_of(blk, rep):
    chips = (blk // 2) * rep
    planes = 1
    while (planes * 2) ** 2 <= chips and (blk // 2) % (planes * 2) == 0:
        planes *= 2
    return planes, blk // 2 // planes


def kernel(
    blk, rep, cap_ref, img_ref, pos_ref, val_ref, closs_ref, iloss_ref, loss_ref,
    caps, imgs, posb, vbuf, rowsend, rowrecv, colsend, colrecv, part, colacc,
    loc_sem, up_sem, down_sem, cap_sem, pos_send, pos_recv, val_send, val_recv,
    own_send, relay_send, img_sem, row_send, row_recv, col_send, col_recv, part_send, part_recv,
):
    U, V = grid_of(blk, rep)
    N = blk * rep
    G = N // U
    n = cap_ref.shape[0]
    ph = n // PIECES
    b, r = lax.axis_index("blk"), lax.axis_index("rep")
    core = b % 2
    u = b // (2 * V)
    v = (b // 2) % V
    me = b * rep + r
    g = me % G

    def member(uu, gg):
        return {"blk": uu * (2 * V) + gg // rep, "rep": gg % rep}

    def device(index):
        return {"blk": index // rep, "rep": index % rep}

    def remote(src, dst, ss, rs, to):
        return pltpu.make_async_remote_copy(
            src_ref=src, dst_ref=dst, send_sem=ss, recv_sem=rs, device_id=to,
            device_id_type=pl.DeviceIdType.MESH,
        )

    barrier = pltpu.get_barrier_semaphore()

    @pl.loop(1, N)
    def _(k):
        pl.semaphore_signal(
            barrier, inc=1, device_id=device((me + k) % N), device_id_type=pl.DeviceIdType.MESH
        )

    pl.semaphore_wait(barrier, N - 1)

    def cap_copy(slot, p, up):
        rows = pl.ds(p * ph, ph)
        to = member(u + 1 if up else u - 1, g)
        return remote(
            caps.at[slot, rows], caps.at[slot, rows],
            (up_sem if up else down_sem).at[slot * PIECES + p], cap_sem.at[slot * PIECES + p], to,
        )

    def own_cap_copy(p, up):
        rows = pl.ds(p * ph, ph)
        to = member(u + 1 if up else u - 1, g)
        return remote(
            cap_ref.at[rows], caps.at[u, rows],
            (up_sem if up else down_sem).at[u * PIECES + p], cap_sem.at[u * PIECES + p], to,
        )

    for p in range(PIECES):
        @pl.when(u < U - 1)
        def _():
            own_cap_copy(p, True).start()

        @pl.when(u > 0)
        def _():
            own_cap_copy(p, False).start()

    def same_core(k):
        vv, rr = (v + k // rep) % V, (r + k % rep) % rep
        return (vv * 2 + core) * rep + rr

    partner = (v * 2 + 1 - core) * rep + r
    M = V * rep

    def own_img_copy(k):
        to = partner if k == 0 else same_core(k)
        return remote(img_ref, imgs.at[g], own_send.at[k], img_sem.at[g], member(u, to))

    def relay_copy(k):
        slot = same_core(k)
        return remote(
            imgs.at[slot], imgs.at[slot], relay_send.at[k], img_sem.at[slot], member(u, partner)
        )

    for k in list(range(1, M)) + [0]:
        own_img_copy(k).start()

    def pos_copy(k):
        return remote(
            pos_ref, posb.at[u], pos_send.at[k], pos_recv.at[u], member((u + k) % U, g)
        )

    for k in range(1, U):
        pos_copy(k).start()

    def val_copy(k):
        return remote(
            val_ref, vbuf.at[me], val_send.at[k], val_recv.at[me], device((me + k) % N)
        )

    @pl.loop(1, N)
    def _(k):
        val_copy(k).start()

    cap_local = pltpu.make_async_copy(cap_ref, caps.at[u], loc_sem.at[0])
    img_local = pltpu.make_async_copy(img_ref, imgs.at[g], loc_sem.at[1])
    cap_local.start()
    img_local.start()
    posb[u] = pos_ref[...]
    vbuf[me] = val_ref[...]

    def pass_on(distance):
        for p in range(PIECES):
            @pl.when(u - distance >= 0)
            def _():
                copy = cap_copy(u - distance, p, True)
                copy.wait_recv()

                @pl.when(u < U - 1)
                def _():
                    copy.start()

            @pl.when(u + distance < U)
            def _():
                copy = cap_copy(u + distance, p, False)
                copy.wait_recv()

                @pl.when(u > 0)
                def _():
                    copy.start()

    @pl.loop(1, N)
    def _(k):
        slot = (me + k) % N
        remote(
            val_ref, vbuf.at[slot], val_send.at[k], val_recv.at[slot], device(slot)
        ).wait_recv()

    for k in range(1, U):
        slot = (u + k) % U
        remote(
            pos_ref, posb.at[slot], pos_send.at[k], pos_recv.at[slot], member(slot, g)
        ).wait_recv()

    eye = lax.broadcasted_iota(jnp.int32, (n, n), 0) == lax.broadcasted_iota(jnp.int32, (n, n), 1)

    def to_column(row):
        return jnp.sum(jnp.where(eye, row, 0.0), axis=1, keepdims=True)

    def to_row(column):
        return jnp.sum(jnp.where(eye, column, 0.0), axis=0, keepdims=True)

    flags = vbuf[:, 0, :].astype(jnp.float32)
    image_total = jnp.sum(jnp.sum(flags, axis=1, keepdims=True), axis=0, keepdims=True)
    starts = lax.broadcasted_iota(jnp.int32, (n, N), 1) * n
    lanes = lax.broadcasted_iota(jnp.int32, (n, n), 1)

    def caption_state(slot):
        target = to_column(posb[slot].astype(jnp.float32)).astype(jnp.int32)
        inside = (target >= starts) & (target < starts + n)
        picked = jnp.dot(
            jnp.where(inside, 1.0, 0.0).astype(jnp.bfloat16), flags.astype(jnp.bfloat16),
            preferred_element_type=jnp.float32,
        )
        start = jnp.sum(jnp.where(inside, starts, 0).astype(jnp.float32), axis=1, keepdims=True)
        low = target - start.astype(jnp.int32)
        ok = jnp.sum(jnp.where(lanes == low, picked, 0.0), axis=1, keepdims=True)
        return target, ok

    image_ok = jnp.concatenate(
        [vbuf[u * G + s].astype(jnp.float32) for s in range(G)], axis=1
    )
    image_ids = u * (G * n) + lax.broadcasted_iota(jnp.int32, (1, G * n), 1)
    colacc[0:1, :] = jnp.full((1, G * n), floor, jnp.float32)
    colacc[1:3, :] = jnp.zeros((2, G * n), jnp.float32)

    if U > 2:
        pass_on(1)
    for k in range(1, M):
        copy = relay_copy(k)
        copy.wait_recv()
        copy.start()
        if k == 2 and U > 2:
            pass_on(2)
    for d in range(2 if M <= 2 else 3, U - 1):
        pass_on(d)
    img_local.wait()
    cap_local.wait()
    for k in range(M):
        slot = partner if k == 0 else (same_core(k) // rep + 1 - 2 * core) * rep + same_core(k) % rep
        remote(
            img_ref, imgs.at[slot], own_send.at[0], img_sem.at[slot], member(u, partner)
        ).wait_recv()

    small = jnp.minimum(u, U - 1 - u)
    side = jnp.where(u < U - 1 - u, 1, -1)

    def slot_at(k):
        near = jnp.where(k % 2 == 1, u - (k + 1) // 2, u + (k + 1) // 2)
        return jnp.where(k <= 2 * small, near, u + side * (k - small))

    def row_copy(slot):
        return remote(
            rowsend.at[slot], rowrecv.at[u], row_send.at[slot], row_recv.at[u], member(slot, g)
        )

    @pl.loop(0, U)
    def _(k):
        slot = slot_at(k)

        @pl.when((slot - u == U - 1) | (u - slot == U - 1))
        def _():
            for p in range(PIECES):
                rows = pl.ds(p * ph, ph)
                remote(
                    caps.at[slot, rows], caps.at[slot, rows], up_sem.at[slot * PIECES + p],
                    cap_sem.at[slot * PIECES + p], member(slot, g),
                ).wait_recv()

        target, ok = caption_state(slot)
        scores = lax.dot_general(
            caps[slot], imgs[...].reshape(G * n, imgs.shape[2]), (((1,), (1,)), ((), ())),
            preferred_element_type=jnp.float32,
        )
        usable = jnp.where(image_ok > 0, scores, very_low)
        row_peak = jnp.maximum(jnp.max(usable, axis=1, keepdims=True), floor)
        row_total = jnp.sum(jnp.exp(usable - row_peak), axis=1, keepdims=True)
        picked = jnp.where(target == image_ids, scores, 0.0)
        row_match = jnp.sum(picked, axis=1, keepdims=True)
        rowsend[slot, 0:1, :] = to_row(row_peak)
        rowsend[slot, 1:2, :] = to_row(row_total)
        rowsend[slot, 2:3, :] = to_row(row_match)

        @pl.when(slot != u)
        def _():
            row_copy(slot).start()

        live = jnp.where(ok > 0, scores, very_low)
        old_peak = colacc[0:1, :]
        peak = jnp.maximum(jnp.max(live, axis=0, keepdims=True), old_peak)
        total = jnp.sum(jnp.exp(live - peak), axis=0, keepdims=True)
        colacc[1:2, :] = colacc[1:2, :] * jnp.exp(old_peak - peak) + total
        colacc[0:1, :] = peak
        colacc[2:3, :] = colacc[2:3, :] + jnp.sum(picked, axis=0, keepdims=True)

    for s in range(G):
        colsend[s, 0:3, :] = colacc[0:3, s * n : (s + 1) * n]

    def col_copy(k):
        slot = (g + k) % G
        return remote(
            colsend.at[slot], colrecv.at[g], col_send.at[k], col_recv.at[g], member(u, slot)
        )

    for k in range(1, G):
        col_copy(k).start()

    rowrecv[u] = rowsend[u]
    colrecv[g] = colsend[g]
    own_target, own_caption_ok = caption_state(u)
    caption_ok = to_row(own_caption_ok)

    def joined(parts, count):
        peak = parts[0, 0:1, :]
        for s in range(1, count):
            peak = jnp.maximum(peak, parts[s, 0:1, :])
        total = jnp.zeros_like(peak)
        match = jnp.zeros_like(peak)
        for s in range(count):
            total += parts[s, 1:2, :] * jnp.exp(parts[s, 0:1, :] - peak)
            match += parts[s, 2:3, :]
        return peak + jnp.log(total) - match

    for k in range(1, U):
        slot = (u + k) % U
        remote(
            rowsend.at[slot], rowrecv.at[slot], row_send.at[slot], row_recv.at[slot],
            member(slot, g),
        ).wait_recv()
    caption_loss = caption_ok * joined(rowrecv, U)
    closs_ref[...] = caption_loss
    for k in range(1, G):
        slot = (g + k) % G
        remote(
            colsend.at[slot], colrecv.at[slot], col_send.at[k], col_recv.at[slot],
            member(u, slot),
        ).wait_recv()
    image_loss = val_ref[...].astype(jnp.float32) * joined(colrecv, G)
    iloss_ref[...] = image_loss
    own_sum = jnp.sum(caption_loss + image_loss, axis=1, keepdims=True)
    part[me] = jnp.broadcast_to(own_sum, (1, 128))

    def part_copy(k):
        return remote(
            part.at[me], part.at[me], part_send.at[k], part_recv.at[me], device((me + k) % N)
        )

    @pl.loop(1, N)
    def _(k):
        part_copy(k).start()

    for d in range(U - 1):
        for p in range(PIECES):
            @pl.when((u - d >= 0) & (u < U - 1))
            def _():
                cap_copy(u - d, p, True).wait_send()

            @pl.when((u + d < U) & (u > 0))
            def _():
                cap_copy(u + d, p, False).wait_send()

    for k in range(M):
        own_img_copy(k).wait_send()
        if k:
            relay_copy(k).wait_send()
    for k in range(1, U):
        pos_copy(k).wait_send()
        row_copy((u + k) % U).wait_send()
    for k in range(1, G):
        col_copy(k).wait_send()

    @pl.loop(1, N)
    def _(k):
        val_copy(k).wait_send()

    @pl.loop(1, N)
    def _(k):
        slot = (me + k) % N
        remote(
            part.at[slot], part.at[slot], part_send.at[k], part_recv.at[slot], device(slot)
        ).wait_recv()

    whole = jnp.sum(part[:, 0, :], axis=0, keepdims=True)
    loss_ref[...] = whole[:, 0:1] / (2.0 * image_total)

    @pl.loop(1, N)
    def _(k):
        part_copy(k).wait_send()


def local(blk, rep, captions, images, positives, valid):
    n, width = captions.shape
    U, V = grid_of(blk, rep)
    N = blk * rep
    G = N // U
    f32, i32 = jnp.float32, jnp.int32
    dma = lambda count: pltpu.SemaphoreType.DMA((count,))
    vmem = pl.BlockSpec(memory_space=pltpu.VMEM)
    caption_loss, image_loss, loss = pl.pallas_call(
        functools.partial(kernel, blk, rep),
        out_shape=(
            jax.ShapeDtypeStruct((1, n), f32),
            jax.ShapeDtypeStruct((1, n), f32),
            jax.ShapeDtypeStruct((1, 1), f32),
        ),
        in_specs=[vmem] * 4,
        out_specs=(vmem,) * 3,
        scratch_shapes=[
            pltpu.VMEM((U, n, width), captions.dtype),
            pltpu.VMEM((G, n, width), images.dtype),
            pltpu.VMEM((U, 1, n), i32),
            pltpu.VMEM((N, 1, n), i32),
            pltpu.VMEM((U, 8, n), f32),
            pltpu.VMEM((U, 8, n), f32),
            pltpu.VMEM((G, 8, n), f32),
            pltpu.VMEM((G, 8, n), f32),
            pltpu.VMEM((N, 1, 128), f32),
            pltpu.VMEM((8, G * n), f32),
            dma(2), dma(U * PIECES), dma(U * PIECES), dma(U * PIECES),
            dma(U), dma(U), dma(N), dma(N),
            dma(V * rep), dma(V * rep), dma(G),
            dma(U), dma(U), dma(G), dma(G), dma(N), dma(N),
        ],
        compiler_params=pltpu.CompilerParams(collective_id=0, has_side_effects=True),
    )(captions, images, positives.reshape(1, n), valid.reshape(1, n))
    return caption_loss.reshape(n), image_loss.reshape(n), loss.reshape(())


def solution(mesh):
    placed = (
        P(("blk", "rep"), None),
        P(("blk", "rep"), None),
        P(("blk", "rep")),
        P(("blk", "rep")),
    )
    return jax.shard_map(
        functools.partial(local, mesh.shape["blk"], mesh.shape["rep"]),
        mesh=mesh,
        in_specs=placed,
        out_specs=(P(("blk", "rep")), P(("blk", "rep")), P()),
        check_vma=False,
    )
```

time: 279 us -> 54.2 us (0.19)
  blocking collectives: 217 us -> 0 us
  Pallas kernels: 0 us -> 49.7 us
  local copies, waits for them, and re-layouts: 22.7 us -> 1.86 us
  between operations: 18.6 us -> 2.4 us
  other arithmetic: 10.2 us -> 0 us
  matrix products: 7.15 us -> 0 us
    unnamed x2 -> x0, blocking collectives: 103 us -> none
    all_gather x7 -> x0, blocking collectives: 75.7 us -> none  [the longest x6 68.3 us: merged(): gathered = jax.tree.map(lambda a: lax.all_gather(a, axis), part)]
    pallas_call x0 -> x1, Pallas kernels: none -> 49.7 us  [local(): pl.pallas_call(functools.partial(kernel, blk, rep), out_shape=(jax.ShapeD...]
    psum x1 -> x0, blocking collectives: 38.5 us -> none  [local(): lax.psum((jnp.sum(caption_loss), jnp.sum(image_loss)), ('blk', 'rep'))]
    gather x2 -> x0, local copies, waits for them, and re-layouts: 18.8 us -> none  [the longest x1 17.4 us: local(): piece_ok = jnp.take(image_flags, all_targets, axis=0)]
    dot_general x1 -> x0, matrix products: 7.15 us -> none  [local(): lax.dot_general(piece, image_block, (((1,), (1,)), ((), ())), preferred_e...]
    reduce_sum x3 -> x0, other arithmetic: 4.69 us -> none  [the longest x1 2.69 us: fold_columns(): column_match = jnp.sum(jnp.where(is_positive, scores, 0.0), axis=0)]
    reduce_max x1 -> x0, other arithmetic: 4.31 us -> none  [fold_columns(): highest = jnp.max(jnp.where(caption_live, scores, very_low), axis=0)]
  transfers between devices with their start and end apart: 1 -> 0, of which waited for: 0 -> 0; matrix products, arithmetic and copies ran while one was open for 8% -> 0% of each run, Pallas kernels for 0% -> 0%
where the time goes in v1:
time: 54.2 us; the launch traced here: 54 us
  Pallas kernels  49.7 us (92%)
  between operations  2.4 us (4%)
  local copies, waits for them, and re-layouts  1.86 us (3%)
    pallas_call x1, Pallas kernels, local(): pl.pallas_call(functools.partial(kernel, blk, rep), out_shape=(jax.ShapeD...  49.7 us
    unnamed x6, local copies, waits for them, and re-layouts  1.86 us

profile of v1, /device:TPU:0, one launch (start us, length us, event | category | flops | bytes accessed | tf_op | source)
XLA Modules:
  0.0 54.0 jit_solution(4957401516886013030)
XLA Ops:
  0.6 49.7 %shard_map.67 = (f32[1,192]{1,0:T(1,128)}, f32[1,192]{1,0:T(1,128)}, f32[1,1]{1,0:T(1,128)}) custom-call(bf16[192,768]{1,0:T(8,128)(2,1)} %cap_ref.1, bf16[192,768]{1,0:T(8,128)(2,1)} %img_ref.1, s32[1,192]{1,0:T(1,128)} %bitcast.5, s32[1,192]{1,0:T(1,128)} %bitcast.6), custom_call_target="tpu_custom_call" | custom-call | tf_op jit(solution)/shard_map/pallas_call | solution.py:369
  50.4 0.0 copy-start.1
  50.4 0.7 %copy-done.1 = f32[1,192]{1,0:T(1,128)S(1)} copy-done((f32[1,192]{1,0:T(1,128)S(1)}, f32[1,192]{1,0:T(1,128)}, u32[]{:S(2)}) %copy-start.1) | copy-done | bytes 792
  51.1 0.0 copy-start
  51.1 0.6 %copy.10 = f32[192]{0:T(256)} copy(f32[192]{0:T(256)S(1)} %bitcast.8) | data formatting | bytes 1536
  51.6 0.1 copy-done
  51.7 0.6 %copy.11 = f32[192]{0:T(256)} copy(f32[192]{0:T(256)S(1)} %bitcast.7) | data formatting | bytes 1536
Async XLA Ops:
  50.4 0.7 %copy-start.1 = (f32[1,192]{1,0:T(1,128)S(1)}, f32[1,192]{1,0:T(1,128)}, u32[]{:S(2)}) copy-start(f32[1,192]{1,0:T(1,128)} %get-tuple-element.6) | copy-start | bytes 2308
  51.1 0.6 %copy-start = (f32[1,192]{1,0:T(1,128)S(1)}, f32[1,192]{1,0:T(1,128)}, u32[]{:S(2)}) copy-start(f32[1,192]{1,0:T(1,128)} %get-tuple-element.7) | copy-start | bytes 2308

commit v2 on v1

--- a/solution.py
+++ b/solution.py
@@ -20,11 +20,19 @@
     return planes, blk // 2 // planes
 
 
+def mod(a, b):
+    return a & (b - 1) if b & (b - 1) == 0 else lax.rem(a, b)
+
+
+def div(a, b):
+    return a >> (b.bit_length() - 1) if b & (b - 1) == 0 else lax.div(a, b)
+
+
 def kernel(
     blk, rep, cap_ref, img_ref, pos_ref, val_ref, closs_ref, iloss_ref, loss_ref,
     caps, imgs, posb, vbuf, rowsend, rowrecv, colsend, colrecv, part, colacc,
-    loc_sem, up_sem, down_sem, cap_sem, pos_send, pos_recv, val_send, val_recv,
-    own_send, relay_send, img_sem, row_send, row_recv, col_send, col_recv, part_send, part_recv,
+    loc_sem, up_sem, down_sem, cap_sem, pos_send, pos_recv, val_send, val_recv, plane_send, plane_recv,
+    own_send, relay_send, corner_send, img_sem, row_send, row_recv, col_send, col_recv, part_send, part_recv,
 ):
     U, V = grid_of(blk, rep)
     N = blk * rep
@@ -32,33 +40,30 @@
     n = cap_ref.shape[0]
     ph = n // PIECES
     b, r = lax.axis_index("blk"), lax.axis_index("rep")
-    core = b % 2
-    u = b // (2 * V)
-    v = (b // 2) % V
+    core = mod(b, 2)
+    u = div(b, 2 * V)
+    v = mod(div(b, 2), V)
     me = b * rep + r
-    g = me % G
+    g = mod(me, G)
 
     def member(uu, gg):
-        return {"blk": uu * (2 * V) + gg // rep, "rep": gg % rep}
-
-    def device(index):
-        return {"blk": index // rep, "rep": index % rep}
+        return uu * G + gg
 
     def remote(src, dst, ss, rs, to):
         return pltpu.make_async_remote_copy(
             src_ref=src, dst_ref=dst, send_sem=ss, recv_sem=rs, device_id=to,
-            device_id_type=pl.DeviceIdType.MESH,
+            device_id_type=pl.DeviceIdType.LOGICAL,
         )
 
     barrier = pltpu.get_barrier_semaphore()
 
-    @pl.loop(1, N)
-    def _(k):
+    near = [member(u, mod(g + k, G)) for k in range(1, G)]
+    near += [member(mod(u + k, U), g) for k in range(1, U)]
+    for to in near:
         pl.semaphore_signal(
-            barrier, inc=1, device_id=device((me + k) % N), device_id_type=pl.DeviceIdType.MESH
-        )
-
-    pl.semaphore_wait(barrier, N - 1)
+            barrier, inc=1, device_id=to, device_id_type=pl.DeviceIdType.LOGICAL
+        )
+    pl.semaphore_wait(barrier, len(near))
 
     def cap_copy(slot, p, up):
         rows = pl.ds(p * ph, ph)
@@ -86,7 +91,7 @@
             own_cap_copy(p, False).start()
 
     def same_core(k):
-        vv, rr = (v + k // rep) % V, (r + k % rep) % rep
+        vv, rr = mod(v + k // rep, V), mod(r + k % rep, rep)
         return (vv * 2 + core) * rep + rr
 
     partner = (v * 2 + 1 - core) * rep + r
@@ -102,12 +107,34 @@
             imgs.at[slot], imgs.at[slot], relay_send.at[k], img_sem.at[slot], member(u, partner)
         )
 
-    for k in list(range(1, M)) + [0]:
+    sides = [k for k in range(1, M) if k < rep or k % rep == 0]
+    corners = [k for k in range(1, M) if k not in sides]
+
+    def corner_copy(k, half):
+        if half == 0:
+            slot, to = same_core(k - k % rep), same_core(k % rep)
+        else:
+            slot, to = same_core(k % rep), same_core(k - k % rep)
+        rows = pl.ds(half * (n // 2), n // 2)
+        return remote(
+            imgs.at[slot, rows], imgs.at[slot, rows], corner_send.at[half * M + k],
+            img_sem.at[half * G + slot], member(u, to),
+        )
+
+    def corner_arrival(k, half):
+        slot = same_core(k)
+        rows = pl.ds(half * (n // 2), n // 2)
+        return remote(
+            imgs.at[slot, rows], imgs.at[slot, rows], corner_send.at[half * M + k],
+            img_sem.at[half * G + slot], member(u, slot),
+        )
+
+    for k in sides + [0]:
         own_img_copy(k).start()
 
     def pos_copy(k):
         return remote(
-            pos_ref, posb.at[u], pos_send.at[k], pos_recv.at[u], member((u + k) % U, g)
+            pos_ref, posb.at[u], pos_send.at[k], pos_recv.at[u], member(mod(u + k, U), g)
         )
 
     for k in range(1, U):
@@ -115,12 +142,18 @@
 
     def val_copy(k):
         return remote(
-            val_ref, vbuf.at[me], val_send.at[k], val_recv.at[me], device((me + k) % N)
-        )
-
-    @pl.loop(1, N)
-    def _(k):
+            val_ref, vbuf.at[me], val_send.at[k], val_recv.at[g], member(u, mod(g + k, G))
+        )
+
+    for k in range(1, G):
         val_copy(k).start()
+
+    def plane_copy(k):
+        rows = pl.ds(u * G, G)
+        return remote(
+            vbuf.at[rows], vbuf.at[rows], plane_send.at[k], plane_recv.at[u],
+            member(mod(u + k, U), g),
+        )
 
     cap_local = pltpu.make_async_copy(cap_ref, caps.at[u], loc_sem.at[0])
     img_local = pltpu.make_async_copy(img_ref, imgs.at[g], loc_sem.at[1])
@@ -149,15 +182,23 @@
                 def _():
                     copy.start()
 
-    @pl.loop(1, N)
-    def _(k):
-        slot = (me + k) % N
-        remote(
-            val_ref, vbuf.at[slot], val_send.at[k], val_recv.at[slot], device(slot)
-        ).wait_recv()
-
-    for k in range(1, U):
-        slot = (u + k) % U
+    for k in range(1, G):
+        slot = mod(g + k, G)
+        remote(
+            val_ref, vbuf.at[u * G + slot], val_send.at[k], val_recv.at[slot], member(u, slot)
+        ).wait_recv()
+    for k in range(1, U):
+        plane_copy(k).start()
+    if U > 2:
+        pass_on(1)
+    for k in range(1, U):
+        slot = mod(u + k, U)
+        rows = pl.ds(slot * G, G)
+        remote(
+            vbuf.at[rows], vbuf.at[rows], plane_send.at[k], plane_recv.at[slot], member(slot, g)
+        ).wait_recv()
+    for k in range(1, U):
+        slot = mod(u + k, U)
         remote(
             pos_ref, posb.at[slot], pos_send.at[k], pos_recv.at[slot], member(slot, g)
         ).wait_recv()
@@ -194,20 +235,25 @@
     colacc[0:1, :] = jnp.full((1, G * n), floor, jnp.float32)
     colacc[1:3, :] = jnp.zeros((2, G * n), jnp.float32)
 
-    if U > 2:
-        pass_on(1)
-    for k in range(1, M):
+    for k in sides:
         copy = relay_copy(k)
         copy.wait_recv()
+        for c in corners:
+            if k == c - c % rep:
+                corner_copy(c, 0).start()
+            if k == c % rep:
+                corner_copy(c, 1).start()
         copy.start()
-        if k == 2 and U > 2:
-            pass_on(2)
-    for d in range(2 if M <= 2 else 3, U - 1):
+    for d in range(2, U - 1):
         pass_on(d)
+    for k in corners:
+        corner_arrival(k, 0).wait_recv()
+        corner_arrival(k, 1).wait_recv()
+        relay_copy(k).start()
     img_local.wait()
     cap_local.wait()
     for k in range(M):
-        slot = partner if k == 0 else (same_core(k) // rep + 1 - 2 * core) * rep + same_core(k) % rep
+        slot = partner if k == 0 else same_core(k) + (1 - 2 * core) * rep
         remote(
             img_ref, imgs.at[slot], own_send.at[0], img_sem.at[slot], member(u, partner)
         ).wait_recv()
@@ -216,7 +262,7 @@
     side = jnp.where(u < U - 1 - u, 1, -1)
 
     def slot_at(k):
-        near = jnp.where(k % 2 == 1, u - (k + 1) // 2, u + (k + 1) // 2)
+        near = jnp.where(mod(k, 2) == 1, u - div(k + 1, 2), u + div(k + 1, 2))
         return jnp.where(k <= 2 * small, near, u + side * (k - small))
 
     def row_copy(slot):
@@ -267,7 +313,7 @@
         colsend[s, 0:3, :] = colacc[0:3, s * n : (s + 1) * n]
 
     def col_copy(k):
-        slot = (g + k) % G
+        slot = mod(g + k, G)
         return remote(
             colsend.at[slot], colrecv.at[g], col_send.at[k], col_recv.at[g], member(u, slot)
         )
@@ -292,7 +338,7 @@
         return peak + jnp.log(total) - match
 
     for k in range(1, U):
-        slot = (u + k) % U
+        slot = mod(u + k, U)
         remote(
             rowsend.at[slot], rowrecv.at[slot], row_send.at[slot], row_recv.at[slot],
             member(slot, g),
@@ -300,7 +346,7 @@
     caption_loss = caption_ok * joined(rowrecv, U)
     closs_ref[...] = caption_loss
     for k in range(1, G):
-        slot = (g + k) % G
+        slot = mod(g + k, G)
         remote(
             colsend.at[slot], colrecv.at[slot], col_send.at[k], col_recv.at[slot],
             member(u, slot),
@@ -312,7 +358,7 @@
 
     def part_copy(k):
         return remote(
-            part.at[me], part.at[me], part_send.at[k], part_recv.at[me], device((me + k) % N)
+            part.at[me], part.at[me], part_send.at[k], part_recv.at[me], mod(me + k, N)
         )
 
     @pl.loop(1, N)
@@ -329,25 +375,29 @@
             def _():
                 cap_copy(u + d, p, False).wait_send()
 
-    for k in range(M):
+    for k in [0] + sides:
         own_img_copy(k).wait_send()
-        if k:
-            relay_copy(k).wait_send()
+    for k in range(1, M):
+        relay_copy(k).wait_send()
+    for k in corners:
+        corner_copy(k, 0).wait_send()
+        corner_copy(k, 1).wait_send()
     for k in range(1, U):
         pos_copy(k).wait_send()
-        row_copy((u + k) % U).wait_send()
+        row_copy(mod(u + k, U)).wait_send()
     for k in range(1, G):
         col_copy(k).wait_send()
+
+    for k in range(1, G):
+        val_copy(k).wait_send()
+    for k in range(1, U):
+        plane_copy(k).wait_send()
 
     @pl.loop(1, N)
     def _(k):
-        val_copy(k).wait_send()
-
-    @pl.loop(1, N)
-    def _(k):
-        slot = (me + k) % N
-        remote(
-            part.at[slot], part.at[slot], part_send.at[k], part_recv.at[slot], device(slot)
+        slot = mod(me + k, N)
+        remote(
+            part.at[slot], part.at[slot], part_send.at[k], part_recv.at[slot], slot
         ).wait_recv()
 
     whole = jnp.sum(part[:, 0, :], axis=0, keepdims=True)
@@ -387,8 +437,8 @@
             pltpu.VMEM((N, 1, 128), f32),
             pltpu.VMEM((8, G * n), f32),
             dma(2), dma(U * PIECES), dma(U * PIECES), dma(U * PIECES),
-            dma(U), dma(U), dma(N), dma(N),
-            dma(V * rep), dma(V * rep), dma(G),
+            dma(U), dma(U), dma(G), dma(G), dma(U), dma(U),
+            dma(V * rep), dma(V * rep), dma(2 * V * rep), dma(2 * G),
             dma(U), dma(U), dma(G), dma(G), dma(N), dma(N),
         ],
         compiler_params=pltpu.CompilerParams(collective_id=0, has_side_effects=True),

time: 54.2 us -> 45.7 us (0.84)
  Pallas kernels: 49.7 us -> 41.3 us
    pallas_call x1, Pallas kernels: 49.7 us -> 41.3 us  [local(): pl.pallas_call(functools.partial(kernel, blk, rep), out_shape=(jax.ShapeD...]
where the time goes in v2:
time: 45.7 us; the launch traced here: 45.6 us
  Pallas kernels  41.3 us (90%)
  between operations  2.4 us (5%)
  local copies, waits for them, and re-layouts  1.86 us (4%)
    pallas_call x1, Pallas kernels, local(): pl.pallas_call(functools.partial(kernel, blk, rep), out_shape=(jax.ShapeD...  41.3 us
    unnamed x6, local copies, waits for them, and re-layouts  1.86 us

profile of v2, /device:TPU:0, one launch (start us, length us, event | category | flops | bytes accessed | tf_op | source)
XLA Modules:
  0.0 45.6 jit_solution(5894648210038484921)
XLA Ops:
  0.6 41.3 %shard_map.67 = (f32[1,192]{1,0:T(1,128)}, f32[1,192]{1,0:T(1,128)}, f32[1,1]{1,0:T(1,128)}) custom-call(bf16[192,768]{1,0:T(8,128)(2,1)} %cap_ref.1, bf16[192,768]{1,0:T(8,128)(2,1)} %img_ref.1, s32[1,192]{1,0:T(1,128)} %bitcast.5, s32[1,192]{1,0:T(1,128)} %bitcast.6), custom_call_target="tpu_custom_call" | custom-call | tf_op jit(solution)/shard_map/pallas_call | solution.py:419
  41.9 0.0 copy-start.1
  41.9 0.7 %copy-done.1 = f32[1,192]{1,0:T(1,128)S(1)} copy-done((f32[1,192]{1,0:T(1,128)S(1)}, f32[1,192]{1,0:T(1,128)}, u32[]{:S(2)}) %copy-start.1) | copy-done | bytes 792
  42.6 0.0 copy-start
  42.6 0.6 %copy.10 = f32[192]{0:T(256)} copy(f32[192]{0:T(256)S(1)} %bitcast.8) | data formatting | bytes 1536
  43.2 0.1 copy-done
  43.2 0.6 %copy.11 = f32[192]{0:T(256)} copy(f32[192]{0:T(256)S(1)} %bitcast.7) | data formatting | bytes 1536
Async XLA Ops:
  41.9 0.7 %copy-start.1 = (f32[1,192]{1,0:T(1,128)S(1)}, f32[1,192]{1,0:T(1,128)}, u32[]{:S(2)}) copy-start(f32[1,192]{1,0:T(1,128)} %get-tuple-element.6) | copy-start | bytes 2308
  42.6 0.6 %copy-start = (f32[1,192]{1,0:T(1,128)S(1)}, f32[1,192]{1,0:T(1,128)}, u32[]{:S(2)}) copy-start(f32[1,192]{1,0:T(1,128)} %get-tuple-element.7) | copy-start | bytes 2308

commit v3 on v2

--- a/solution.py
+++ b/solution.py
@@ -81,6 +81,29 @@
             (up_sem if up else down_sem).at[u * PIECES + p], cap_sem.at[u * PIECES + p], to,
         )
 
+    def pos_copy(k):
+        return remote(
+            pos_ref, posb.at[u], pos_send.at[k], pos_recv.at[u], member(mod(u + k, U), g)
+        )
+
+    for k in range(1, U):
+        pos_copy(k).start()
+
+    def val_copy(k):
+        return remote(
+            val_ref, vbuf.at[me], val_send.at[k], val_recv.at[g], member(u, mod(g + k, G))
+        )
+
+    for k in range(1, G):
+        val_copy(k).start()
+
+    def plane_copy(k):
+        rows = pl.ds(u * G, G)
+        return remote(
+            vbuf.at[rows], vbuf.at[rows], plane_send.at[k], plane_recv.at[u],
+            member(mod(u + k, U), g),
+        )
+
     for p in range(PIECES):
         @pl.when(u < U - 1)
         def _():
@@ -132,29 +155,6 @@
     for k in sides + [0]:
         own_img_copy(k).start()
 
-    def pos_copy(k):
-        return remote(
-            pos_ref, posb.at[u], pos_send.at[k], pos_recv.at[u], member(mod(u + k, U), g)
-        )
-
-    for k in range(1, U):
-        pos_copy(k).start()
-
-    def val_copy(k):
-        return remote(
-            val_ref, vbuf.at[me], val_send.at[k], val_recv.at[g], member(u, mod(g + k, G))
-        )
-
-    for k in range(1, G):
-        val_copy(k).start()
-
-    def plane_copy(k):
-        rows = pl.ds(u * G, G)
-        return remote(
-            vbuf.at[rows], vbuf.at[rows], plane_send.at[k], plane_recv.at[u],
-            member(mod(u + k, U), g),
-        )
-
     cap_local = pltpu.make_async_copy(cap_ref, caps.at[u], loc_sem.at[0])
     img_local = pltpu.make_async_copy(img_ref, imgs.at[g], loc_sem.at[1])
     cap_local.start()
@@ -191,50 +191,6 @@
         plane_copy(k).start()
     if U > 2:
         pass_on(1)
-    for k in range(1, U):
-        slot = mod(u + k, U)
-        rows = pl.ds(slot * G, G)
-        remote(
-            vbuf.at[rows], vbuf.at[rows], plane_send.at[k], plane_recv.at[slot], member(slot, g)
-        ).wait_recv()
-    for k in range(1, U):
-        slot = mod(u + k, U)
-        remote(
-            pos_ref, posb.at[slot], pos_send.at[k], pos_recv.at[slot], member(slot, g)
-        ).wait_recv()
-
-    eye = lax.broadcasted_iota(jnp.int32, (n, n), 0) == lax.broadcasted_iota(jnp.int32, (n, n), 1)
-
-    def to_column(row):
-        return jnp.sum(jnp.where(eye, row, 0.0), axis=1, keepdims=True)
-
-    def to_row(column):
-        return jnp.sum(jnp.where(eye, column, 0.0), axis=0, keepdims=True)
-
-    flags = vbuf[:, 0, :].astype(jnp.float32)
-    image_total = jnp.sum(jnp.sum(flags, axis=1, keepdims=True), axis=0, keepdims=True)
-    starts = lax.broadcasted_iota(jnp.int32, (n, N), 1) * n
-    lanes = lax.broadcasted_iota(jnp.int32, (n, n), 1)
-
-    def caption_state(slot):
-        target = to_column(posb[slot].astype(jnp.float32)).astype(jnp.int32)
-        inside = (target >= starts) & (target < starts + n)
-        picked = jnp.dot(
-            jnp.where(inside, 1.0, 0.0).astype(jnp.bfloat16), flags.astype(jnp.bfloat16),
-            preferred_element_type=jnp.float32,
-        )
-        start = jnp.sum(jnp.where(inside, starts, 0).astype(jnp.float32), axis=1, keepdims=True)
-        low = target - start.astype(jnp.int32)
-        ok = jnp.sum(jnp.where(lanes == low, picked, 0.0), axis=1, keepdims=True)
-        return target, ok
-
-    image_ok = jnp.concatenate(
-        [vbuf[u * G + s].astype(jnp.float32) for s in range(G)], axis=1
-    )
-    image_ids = u * (G * n) + lax.broadcasted_iota(jnp.int32, (1, G * n), 1)
-    colacc[0:1, :] = jnp.full((1, G * n), floor, jnp.float32)
-    colacc[1:3, :] = jnp.zeros((2, G * n), jnp.float32)
-
     for k in sides:
         copy = relay_copy(k)
         copy.wait_recv()
@@ -250,6 +206,50 @@
         corner_arrival(k, 0).wait_recv()
         corner_arrival(k, 1).wait_recv()
         relay_copy(k).start()
+    for k in range(1, U):
+        slot = mod(u + k, U)
+        rows = pl.ds(slot * G, G)
+        remote(
+            vbuf.at[rows], vbuf.at[rows], plane_send.at[k], plane_recv.at[slot], member(slot, g)
+        ).wait_recv()
+    for k in range(1, U):
+        slot = mod(u + k, U)
+        remote(
+            pos_ref, posb.at[slot], pos_send.at[k], pos_recv.at[slot], member(slot, g)
+        ).wait_recv()
+
+    eye = lax.broadcasted_iota(jnp.int32, (n, n), 0) == lax.broadcasted_iota(jnp.int32, (n, n), 1)
+
+    def to_column(row):
+        return jnp.sum(jnp.where(eye, row, 0.0), axis=1, keepdims=True)
+
+    def to_row(column):
+        return jnp.sum(jnp.where(eye, column, 0.0), axis=0, keepdims=True)
+
+    flags = vbuf[:, 0, :].astype(jnp.float32)
+    image_total = jnp.sum(jnp.sum(flags, axis=1, keepdims=True), axis=0, keepdims=True)
+    starts = lax.broadcasted_iota(jnp.int32, (n, N), 1) * n
+    lanes = lax.broadcasted_iota(jnp.int32, (n, n), 1)
+
+    def caption_state(slot):
+        target = to_column(posb[slot].astype(jnp.float32)).astype(jnp.int32)
+        inside = (target >= starts) & (target < starts + n)
+        picked = jnp.dot(
+            jnp.where(inside, 1.0, 0.0).astype(jnp.bfloat16), flags.astype(jnp.bfloat16),
+            preferred_element_type=jnp.float32,
+        )
+        start = jnp.sum(jnp.where(inside, starts, 0).astype(jnp.float32), axis=1, keepdims=True)
+        low = target - start.astype(jnp.int32)
+        ok = jnp.sum(jnp.where(lanes == low, picked, 0.0), axis=1, keepdims=True)
+        return target, ok
+
+    image_ok = jnp.concatenate(
+        [vbuf[u * G + s].astype(jnp.float32) for s in range(G)], axis=1
+    )
+    image_ids = u * (G * n) + lax.broadcasted_iota(jnp.int32, (1, G * n), 1)
+    colacc[0:1, :] = jnp.full((1, G * n), floor, jnp.float32)
+    colacc[1:3, :] = jnp.zeros((2, G * n), jnp.float32)
+
     img_local.wait()
     cap_local.wait()
     for k in range(M):

time: 45.7 us -> 43.9 us (0.961)
  Pallas kernels: 41.3 us -> 39.4 us
    pallas_call x1, Pallas kernels: 41.3 us -> 39.4 us  [local(): pl.pallas_call(functools.partial(kernel, blk, rep), out_shape=(jax.ShapeD...]
where the time goes in v3:
time: 43.9 us; the launch traced here: 43.7 us
  Pallas kernels  39.4 us (90%)
  between operations  2.4 us (5%)
  local copies, waits for them, and re-layouts  1.86 us (4%)
    pallas_call x1, Pallas kernels, local(): pl.pallas_call(functools.partial(kernel, blk, rep), out_shape=(jax.ShapeD...  39.4 us
    unnamed x6, local copies, waits for them, and re-layouts  1.86 us

profile of v3, /device:TPU:0, one launch (start us, length us, event | category | flops | bytes accessed | tf_op | source)
XLA Modules:
  0.0 43.7 jit_solution(9273966478487488997)
XLA Ops:
  0.6 39.4 %shard_map.67 = (f32[1,192]{1,0:T(1,128)}, f32[1,192]{1,0:T(1,128)}, f32[1,1]{1,0:T(1,128)}) custom-call(bf16[192,768]{1,0:T(8,128)(2,1)} %cap_ref.1, bf16[192,768]{1,0:T(8,128)(2,1)} %img_ref.1, s32[1,192]{1,0:T(1,128)} %bitcast.5, s32[1,192]{1,0:T(1,128)} %bitcast.6), custom_call_target="tpu_custom_call" | custom-call | tf_op jit(solution)/shard_map/pallas_call | solution.py:419
  40.1 0.0 copy-start.1
  40.1 0.7 %copy-done.1 = f32[1,192]{1,0:T(1,128)S(1)} copy-done((f32[1,192]{1,0:T(1,128)S(1)}, f32[1,192]{1,0:T(1,128)}, u32[]{:S(2)}) %copy-start.1) | copy-done | bytes 792
  40.7 0.0 copy-start
  40.7 0.6 %copy.10 = f32[192]{0:T(256)} copy(f32[192]{0:T(256)S(1)} %bitcast.8) | data formatting | bytes 1536
  41.3 0.1 copy-done
  41.4 0.6 %copy.11 = f32[192]{0:T(256)} copy(f32[192]{0:T(256)S(1)} %bitcast.7) | data formatting | bytes 1536
Async XLA Ops:
  40.1 0.7 %copy-start.1 = (f32[1,192]{1,0:T(1,128)S(1)}, f32[1,192]{1,0:T(1,128)}, u32[]{:S(2)}) copy-start(f32[1,192]{1,0:T(1,128)} %get-tuple-element.6) | copy-start | bytes 2308
  40.7 0.6 %copy-start = (f32[1,192]{1,0:T(1,128)S(1)}, f32[1,192]{1,0:T(1,128)}, u32[]{:S(2)}) copy-start(f32[1,192]{1,0:T(1,128)} %get-tuple-element.7) | copy-start | bytes 2308
